TPU v7x, 32 devices: a whole 2x2x4 slice. The times are simulated.
32 devices in a mesh: rows: 8 (over z, y), cols: 4 (over x, core).
Axes of the slice: x: 2, y: 2, z: 4, core: 2. Of those that a mesh axis runs over, the one named last changes fastest.
Arguments:
- w_gate: float32 [2048, 8192], P('rows', 'cols'), may hold values from -0.1875 to 0.1875
- first_gate: float32 [2048, 8192], P('rows', 'cols'), may hold values from -6 to 6
- second_gate: float32 [2048, 8192], P('rows', 'cols'), may hold values from 0.1 to 10
- w_up: float32 [2048, 8192], P('rows', 'cols'), may hold values from -0.1875 to 0.1875
- first_up: float32 [2048, 8192], P('rows', 'cols'), may hold values from -6 to 6
- second_up: float32 [2048, 8192], P('rows', 'cols'), may hold values from 0.1 to 10
- norm_train: float32 [2048], P(('rows', 'cols')), may hold values from 0.25 to 1.75
- norm_step: float32 [2048], P(('rows', 'cols')), may hold values from -0.3 to 0.3
Outputs:
- ready_gate: bfloat16 [2048, 8192], P(None, 'cols')
- ready_up: bfloat16 [2048, 8192], P(None, 'cols')
- column_gate: float32 [8192], P('cols')
- column_up: float32 [8192], P('cols')
- serve_norm: bfloat16 [2048], replicated
- latest_gate: float32 [2048, 8192], P('rows', 'cols')
- latest_up: float32 [2048, 8192], P('rows', 'cols')
All inputs are finite; a program needn't handle non-finite values. Where the computation divides by a largest or mean magnitude, that divisor is 1e-20 or more.
Results may differ from a plain program's by a relative error of at most 0.001.
Values may be sent and summed in bfloat16 or wider, within the bound.
A program may use at most 128 MiB of HBM per device.

v0:
```python
import jax
import jax.numpy as jnp
from jax import lax
from jax.sharding import PartitionSpec as P

D_MODEL = 2048


learn_rate = 0.01
decay_rate = 0.1
tiny_value = 1e-08


def local(w_gate, first_gate, second_gate, w_up, first_up, second_up, norm_train, norm_step):
    latest_gate = w_gate - learn_rate * (
        first_gate / (jnp.sqrt(second_gate) + tiny_value) + decay_rate * w_gate
    )
    latest_up = w_up - learn_rate * (
        first_up / (jnp.sqrt(second_up) + tiny_value) + decay_rate * w_up
    )
    total_gate, total_up = lax.psum(
        (jnp.sum(jnp.abs(latest_gate), axis=0), jnp.sum(jnp.abs(latest_up), axis=0)), "rows"
    )
    column_gate = total_gate / D_MODEL
    column_up = total_up / D_MODEL
    narrow_gate, narrow_up = (
        (latest_gate / column_gate).astype(jnp.bfloat16),
        (latest_up / column_up).astype(jnp.bfloat16),
    )
    ready_gate, ready_up = (
        lax.all_gather(narrow_gate, "rows", axis=0, tiled=True),
        lax.all_gather(narrow_up, "rows", axis=0, tiled=True),
    )
    serve_norm = lax.all_gather(
        (norm_train + norm_step).astype(jnp.bfloat16), ("rows", "cols"), axis=0, tiled=True
    )
    return (ready_gate, ready_up, column_gate, column_up, serve_norm, latest_gate, latest_up)


def solution(mesh):
    placed = (
        P("rows", "cols"),
        P("rows", "cols"),
        P("rows", "cols"),
        P("rows", "cols"),
        P("rows", "cols"),
        P("rows", "cols"),
        P(("rows", "cols")),
        P(("rows", "cols")),
    )
    return jax.shard_map(
        local,
        mesh=mesh,
        in_specs=placed,
        out_specs=(
            P(None, "cols"),
            P(None, "cols"),
            P("cols"),
            P("cols"),
            P(),
            P("rows", "cols"),
            P("rows", "cols"),
        ),
        check_vma=False,
    )
```

profile of v0, /device:TPU:0, one launch (start us, length us, event | category | flops | bytes accessed | tf_op | source)
XLA Modules:
  0.0 327.5 jit_solution(13651855126006088552)
XLA Ops:
  7.2 0.0 all-gather.5.cloned.1.call-start
  7.2 8.2 %abs_reduce_fusion = (f32[2048]{0:T(1024)S(1)}, f32[256,2048]{1,0:T(8,128)S(1)}, f32[2048]{0:T(1024)S(1)}, f32[256,2048]{1,0:T(8,128)}) fusion(f32[256,2048]{1,0:T(8,128)} %param.11, f32[256,2048]{1,0:T(8,128)} %param.12, f32[256,2048]{1,0:T(8,128)} %param.13, f32[256,2048]{1,0:T(8,128)} %param.8, f32[256,2048]{1,0:T(8,128)} %param.9, f32[256,2048]{1,0:T(8,128)} %param.10), kind=kLoop, calls=%fused_computation.1 | loop fusion | flops 8384512 | bytes 16793600 | tf_op jit(solution)/shard_map/reduce_sum | solution.py:22
  15.4 0.0 copy-start
  15.4 38.9 %all-reduce.1 = (f32[2048]{0:T(1024)S(1)}, f32[2048]{0:T(1024)S(1)}) all-reduce(f32[2048]{0:T(1024)S(1)} %get-tuple-element.13, f32[2048]{0:T(1024)S(1)} %get-tuple-element.9), channel_id=1, replica_groups=mesh['rows'=8,'cols'=4] {'rows'}, use_global_device_ids=true, to_apply=%region_1.0 | all-reduce | flops 4096 | bytes 32768 | tf_op jit(solution)/shard_map/psum | solution.py:21
  54.3 0.0 copy-start.1
  54.3 1.2 divide_convert_fusion
  55.4 0.0 all-gather.5.cloned.1.call-update
  55.4 0.0 copy-done
  55.4 0.0 copy-done.1
  55.5 0.0 all-gather.3.cloned.1.call-start
  55.5 0.0 copy-start.2
  55.5 0.0 copy-start.3
  55.5 0.0 copy-start.4
  55.6 2.8 divide_convert_fusion.1
  58.3 0.0 all-gather.3.cloned.1.call-update
  58.3 0.0 copy-done.2
  58.4 0.0 copy-done.3
  58.4 0.0 copy-done.4
  58.4 0.2 dynamic-update-slice
  58.6 40.6 %all-reduce = bf16[2048]{0:T(1024)(128)(2,1)} all-reduce(bf16[2048]{0:T(1024)(128)(2,1)S(1)} %dynamic-update-slice), channel_id=1, replica_groups=mesh['rows'=8,'cols'=4] {'rows','cols'}, use_global_device_ids=true, to_apply=%add | all-reduce | flops 2048 | bytes 8192
  99.3 79.1 %all-gather.5.cloned.1.call-done = bf16[2048,2048]{1,0:T(8,128)(2,1)} async-done(((bf16[256,2048]{1,0:T(8,128)(2,1)}), bf16[2048,2048]{1,0:T(8,128)(2,1)}) %all-gather.5.cloned.1.call-update) | async-done | bytes 8388624 | tf_op jit(solution)/shard_map/all_gather | solution.py:32
  178.4 125.4 %all-gather.3.cloned.1.call-done = bf16[2048,2048]{1,0:T(8,128)(2,1)} async-done(((bf16[256,2048]{1,0:T(8,128)(2,1)}), bf16[2048,2048]{1,0:T(8,128)(2,1)}) %all-gather.3.cloned.1.call-update) | async-done | bytes 8388624 | tf_op jit(solution)/shard_map/all_gather | solution.py:31
  303.8 8.4 %copy.18 = bf16[2048,2048]{1,0:T(8,128)(2,1)} copy(bf16[2048,2048]{1,0:T(8,128)(2,1)} %all-gather.3.cloned.1.call-done) | data formatting | bytes 16777216
  312.2 8.4 %copy.19 = bf16[2048,2048]{1,0:T(8,128)(2,1)} copy(bf16[2048,2048]{1,0:T(8,128)(2,1)} %all-gather.5.cloned.1.call-done) | data formatting | bytes 16777216
  (4 shorter events, 0.0 us)
Async XLA Ops:
  7.2 171.2 %all-gather.5.cloned.1.call-start = ((), (), s32[]{:S(2)}) async-start(), calls=%async_computation.1 | async-start | bytes 9437184 | tf_op jit(solution)/shard_map/all_gather | solution.py:32
  15.4 40.1 %copy-start = (f32[256,2048]{1,0:T(8,128)}, f32[256,2048]{1,0:T(8,128)S(1)}, u32[]{:S(2)}) copy-start(f32[256,2048]{1,0:T(8,128)S(1)} %get-tuple-element.28) | copy-start | bytes 6291460
  54.3 1.2 copy-start.1
  55.5 248.3 %all-gather.3.cloned.1.call-start = ((), (), s32[]{:S(2)}) async-start(), calls=%async_computation | async-start | bytes 9437184 | tf_op jit(solution)/shard_map/all_gather | solution.py:31
  55.5 2.8 copy-start.2
  55.5 2.8 copy-start.3
  55.5 2.8 copy-start.4
Sparse Core Ops, SparseCore 0:
  55.6 122.7 all-gather.4
  181.1 122.6 all-gather.2
where the time goes:
time: 328 us; the launch traced here: 327 us
  waiting for transfers between devices  204 us (62%)
  blocking collectives  79.5 us (24%)
  local copies, waits for them, and re-layouts  17.2 us (5%)
  between operations  14.1 us (4%)
  other arithmetic  12.1 us (4%)
    all_gather x1, waiting for transfers between devices, local(): lax.all_gather(narrow_gate, 'rows', axis=0, tiled=True)  125 us
    all_gather x1, waiting for transfers between devices, local(): lax.all_gather(narrow_up, 'rows', axis=0, tiled=True)  79.1 us
    unnamed x1, blocking collectives  40.6 us
    psum x1, blocking collectives, local(): lax.psum((jnp.sum(jnp.abs(latest_gate), axis=0), jnp.sum(jnp.abs(latest_u...  38.9 us
    unnamed x14, local copies, waits for them, and re-layouts  17.2 us
    reduce_sum x1, other arithmetic, local(): jnp.sum(jnp.abs(latest_up), axis=0)  8.17 us
  transfers between devices with their start and end apart: 2, of which 2 were waited for; matrix products, arithmetic and copies ran while one was open for 1% of the time, Pallas kernels for 0%

commit v1 on v0

v1 whole, which is shorter than its diff:
```python
import functools

import jax
import jax.numpy as jnp
from jax import lax
from jax.experimental import pallas as pl
from jax.experimental.pallas import tpu as pltpu
from jax.sharding import PartitionSpec as P

MESH = pl.DeviceIdType.MESH

learn_rate = 0.01
decay_rate = 0.1
tiny_value = 1e-08

PARTS = 4
SLAB = 32


def stepped(w, first, second):
    return w - learn_rate * (first / (jnp.sqrt(second) + tiny_value) + decay_rate * w)


def kernel(
    n_rows, n_cols, depth,
    w_g, f_g, s_g, w_u, f_u, s_u, norm_ref,
    ready, column, served, latest,
    held, sums, norms, in_sem, sum_send, sum_recv, norm_send, norm_recv, send_sem, recv_sem,
):
    row, col = lax.axis_index("rows"), lax.axis_index("cols")
    z, y = row // 2, lax.rem(row, 2)
    across = z * 2 + (1 - y)
    half = z // 2
    is_outer = lax.rem(z + half, 2) == 0
    out_z, in_z = half * 3, 1 + half
    far_in_z, far_out_z = 2 - half, 3 - half * 3
    share, width = latest.shape[1], latest.shape[2] // PARTS
    pieces = 2 * PARTS
    devices = n_rows * n_cols
    me = row * n_cols + col
    sources = ((w_g, f_g, s_g), (w_u, f_u, s_u))

    def cols_of(k):
        if isinstance(k, int):
            return pl.ds((k % PARTS) * width, width)
        return pl.ds(pl.multiple_of(lax.rem(k, PARTS) * width, width), width)

    def load(k):
        copies = [
            pltpu.make_async_copy(
                ref.at[:, cols_of(k)], held.at[i, k // PARTS, :, cols_of(k)], in_sem.at[i, k]
            )
            for i, ref in enumerate(sources[k // PARTS])
        ]
        return copies

    for k in range(2):
        for c in load(k):
            c.start()

    barrier = pltpu.get_barrier_semaphore()

    def greet(i, carry):
        other = lax.rem(me + i, devices)
        pl.semaphore_signal(
            barrier, inc=1, device_id=(other // n_cols, lax.rem(other, n_cols)), device_id_type=MESH
        )
        return carry

    lax.fori_loop(1, devices, greet, 0)

    lane = lax.broadcasted_iota(jnp.int32, norm_ref.shape, 1)
    low, high = lax.rem(me, 2) * 64, lax.rem(me, 2) * 64 + 64
    norms[me] = jnp.where((lane >= low) & (lane < high), norm_ref[...], 0.0)

    def adam(k):
        for c in load(k):
            c.wait()
        w, cs = k // PARTS, cols_of(k)

        def step(r, total):
            rs = pl.ds(pl.multiple_of(r * SLAB, SLAB), SLAB)
            new = stepped(held[0, w, rs, cs], held[1, w, rs, cs], held[2, w, rs, cs])
            latest[w, rs, cs] = new
            return total + jnp.sum(jnp.abs(new).reshape(SLAB // 8, 8, width), axis=0)

        total = lax.fori_loop(0, share // SLAB, step, jnp.zeros((8, width), jnp.float32))
        sums[k, row] = jnp.sum(total, axis=0, keepdims=True)

    def sum_copy(k, i):
        other = lax.rem(row + i, n_rows)
        return pltpu.make_async_remote_copy(
            src_ref=sums.at[k, row], dst_ref=sums.at[k, row],
            send_sem=sum_send.at[k, other], recv_sem=sum_recv.at[k, row],
            device_id=(other, col), device_id_type=MESH,
        )

    def sum_arrival(k, i):
        other = lax.rem(row + i, n_rows)
        return pltpu.make_async_remote_copy(
            src_ref=sums.at[k, other], dst_ref=sums.at[k, other],
            send_sem=sum_send.at[k, other], recv_sem=sum_recv.at[k, other],
            device_id=(other, col), device_id_type=MESH,
        )

    def scale(k):
        for i in range(1, n_rows):
            sum_arrival(k, i).wait_recv()
        w, cs = k // PARTS, cols_of(k)
        mean = jnp.sum(sums[k], axis=0) / depth
        column[w, :, cs] = mean

        def step(r, carry):
            rs = pl.ds(pl.multiple_of(r * SLAB, SLAB), SLAB)
            to = pl.ds(pl.multiple_of(row * share + r * SLAB, SLAB), SLAB)
            ready[w, to, cs] = (latest[w, rs, cs] / mean).astype(jnp.bfloat16)
            return carry

        lax.fori_loop(0, share // SLAB, step, 0)

    def block(source, k, link, slot, target):
        w = k // PARTS
        ref = ready.at[w, pl.ds(pl.multiple_of(source * share, share), share), cols_of(k)]
        return pltpu.make_async_remote_copy(
            src_ref=ref, dst_ref=ref,
            send_sem=send_sem.at[link, slot, k], recv_sem=recv_sem.at[source, k],
            device_id=(target, col), device_id_type=MESH,
        )

    def arrived(source, k):
        block(source, k, 0, 0, across).wait_recv()

    away = out_z * 2 + y
    near = in_z * 2 + y
    far_near, far_away = far_in_z * 2 + y, far_out_z * 2 + y
    near_across = in_z * 2 + (1 - y)
    away_across = out_z * 2 + (1 - y)
    far_near_across, far_away_across = far_in_z * 2 + (1 - y), far_out_z * 2 + (1 - y)

    partner = jnp.where(is_outer, near, away)

    def send_own(k):
        block(row, k, 1, 0, partner).start()
        block(row, k, 0, 0, across).start()

        @pl.when(jnp.logical_not(is_outer))
        def _():
            block(row, k, 2, 0, far_near).start()

    LAG = 2
    for k in range(pieces + LAG + 2):
        if k < pieces:
            if k + 2 < pieces:
                for c in load(k + 2):
                    c.start()
            adam(k)
        if k == 1:
            pl.semaphore_wait(barrier, devices - 1)
        if 1 <= k <= pieces:
            for i in range(1, n_rows):
                sum_copy(k - 1, i).start()
        if LAG <= k - 1 < pieces + LAG:
            scale(k - 1 - LAG)
        if 0 <= k - 2 - LAG:
            send_own(k - 2 - LAG)

    def norm_copy(i):
        other = lax.rem(me + i, devices)
        return pltpu.make_async_remote_copy(
            src_ref=norms.at[me], dst_ref=norms.at[me],
            send_sem=norm_send.at[other], recv_sem=norm_recv.at[me],
            device_id=(other // n_cols, lax.rem(other, n_cols)), device_id_type=MESH,
        )

    def norm_arrival(i):
        other = lax.rem(me + i, devices)
        return pltpu.make_async_remote_copy(
            src_ref=norms.at[other], dst_ref=norms.at[other],
            send_sem=norm_send.at[other], recv_sem=norm_recv.at[other],
            device_id=(other // n_cols, lax.rem(other, n_cols)), device_id_type=MESH,
        )

    def loop(lo, hi, f):
        def body(i, carry):
            f(i)
            return carry

        lax.fori_loop(lo, hi, body, 0)

    loop(1, devices, lambda i: norm_copy(i).start())

    @pl.when(is_outer)
    def _():
        def one(k):
            arrived(near, k)

            @pl.when(k < PARTS)
            def _():
                block(near, k, 0, 1, across).start()

            arrived(across, k)
            block(across, k, 1, 1, near).start()

        loop(0, pieces, one)

        def two(k):
            arrived(far_near, k)
            block(far_near, k, 0, 2, across).start()

        loop(0, pieces, two)

        def three(k):
            arrived(far_away, k)
            block(far_away, k, 0, 3, across).start()

        loop(0, pieces, three)

        def rest(k):
            arrived(near_across, k)
            arrived(far_near_across, k)
            arrived(far_away_across, k)
            for slot in (0, 2, 3):
                block(row, k, 0, slot, across).wait_send()
            for slot in (0, 1):
                block(row, k, 1, slot, near).wait_send()

            @pl.when(k < PARTS)
            def _():
                block(row, k, 0, 1, across).wait_send()

        loop(0, pieces, rest)

    @pl.when(jnp.logical_not(is_outer))
    def _():
        def one(k):
            arrived(away, k)
            block(away, k, 2, 1, far_near).start()
            arrived(far_near, k)
            block(far_near, k, 1, 1, away).start()
            arrived(across, k)

        loop(0, pieces, one)

        def two(k):
            block(across, k, 2, 2, far_near).start()
            arrived(far_away, k)
            block(far_away, k, 1, 2, away).start()
            block(far_away, k, 0, 1, across).start()

        loop(0, pieces, two)
        loop(PARTS, pieces, lambda k: block(across, k, 1, 3, away).start())

        def rest(k):
            arrived(away_across, k)
            arrived(far_near_across, k)
            arrived(far_away_across, k)
            for slot in (0, 1):
                block(row, k, 0, slot, across).wait_send()
            for slot in (0, 1, 2):
                block(row, k, 1, slot, away).wait_send()
                block(row, k, 2, slot, far_near).wait_send()

            @pl.when(k >= PARTS)
            def _():
                block(row, k, 1, 3, away).wait_send()

        loop(0, pieces, rest)

    for k in range(pieces):
        loop(1, n_rows, lambda i: sum_copy(k, i).wait_send())
    loop(1, devices, lambda i: (norm_copy(i).wait_send(), norm_arrival(i).wait_recv()))
    for i in range(devices // 2):
        served[pl.ds(i, 1), :] = norms[2 * i][0:1] + norms[2 * i + 1][0:1]


def fused(n_rows, n_cols, w_gate, first_gate, second_gate, w_up, first_up, second_up, norm_train, norm_step):
    share, width = w_gate.shape
    depth = share * n_rows
    pieces = 2 * PARTS
    devices = n_rows * n_cols
    norm = norm_train + norm_step
    norm = jnp.broadcast_to(jnp.concatenate([norm, norm])[None, :], (8, 128))
    vmem = pl.BlockSpec(memory_space=pltpu.VMEM)
    dma = pltpu.SemaphoreType.DMA
    ready, column, served, latest = pl.pallas_call(
        functools.partial(kernel, n_rows, n_cols, depth),
        out_shape=[
            pltpu.VMEM((2, depth, width), jnp.bfloat16),
            pltpu.VMEM((2, 1, width), jnp.float32),
            pltpu.VMEM((devices // 2, 128), jnp.float32),
            pltpu.VMEM((2, share, width), jnp.float32),
        ],
        in_specs=[pl.BlockSpec(memory_space=pltpu.HBM)] * 6 + [vmem],
        out_specs=[vmem] * 4,
        scratch_shapes=[
            pltpu.VMEM((3, 2, share, width), jnp.float32),
            pltpu.VMEM((pieces, n_rows, 1, width // PARTS), jnp.float32),
            pltpu.VMEM((devices, 8, 128), jnp.float32),
            dma((3, pieces)),
            dma((pieces, n_rows)),
            dma((pieces, n_rows)),
            dma((devices,)),
            dma((devices,)),
            dma((3, 4, pieces)),
            dma((n_rows, pieces)),
        ],
        compiler_params=pltpu.CompilerParams(
            collective_id=0, has_side_effects=True, vmem_limit_bytes=40 * 2**20
        ),
        name="fused",
    )(w_gate, first_gate, second_gate, w_up, first_up, second_up, norm)
    return (
        ready[0], ready[1], column[0, 0], column[1, 0],
        served.reshape(-1).astype(jnp.bfloat16), latest[0], latest[1],
    )


def plain(n_rows, n_cols, w_gate, first_gate, second_gate, w_up, first_up, second_up, norm_train, norm_step):
    latest = [stepped(w_gate, first_gate, second_gate), stepped(w_up, first_up, second_up)]
    totals = lax.psum(tuple(jnp.sum(jnp.abs(a), axis=0) for a in latest), "rows")
    columns = [t / (w_gate.shape[0] * n_rows) for t in totals]
    ready = [
        lax.all_gather((a / c).astype(jnp.bfloat16), "rows", axis=0, tiled=True)
        for a, c in zip(latest, columns)
    ]
    served = lax.all_gather(
        (norm_train + norm_step).astype(jnp.bfloat16), ("rows", "cols"), axis=0, tiled=True
    )
    return (*ready, *columns, served, *latest)


def solution(mesh):
    n_rows, n_cols = mesh.shape["rows"], mesh.shape["cols"]
    body = fused if (n_rows, n_cols) == (8, 4) else plain
    placed = (P("rows", "cols"),) * 6 + (P(("rows", "cols")),) * 2
    return jax.shard_map(
        functools.partial(body, n_rows, n_cols),
        mesh=mesh,
        in_specs=placed,
        out_specs=(
            P(None, "cols"), P(None, "cols"), P("cols"), P("cols"), P(),
            P("rows", "cols"), P("rows", "cols"),
        ),
        check_vma=False,
    )
```

time: 328 us -> 190 us (0.58)
  waiting for transfers between devices: 204 us -> 0 us
  Pallas kernels: 0 us -> 178 us
  blocking collectives: 79.5 us -> 0 us
  between operations: 14.1 us -> 0.64 us
  other arithmetic: 12.1 us -> 1.35 us
  local copies, waits for them, and re-layouts: 17.2 us -> 9.96 us
    all_gather x2 -> x0, waiting for transfers between devices: 204 us -> none  [the longest x1 125 us: local(): lax.all_gather(narrow_gate, 'rows', axis=0, tiled=True)]
    pallas_call x0 -> x1, Pallas kernels: none -> 178 us  [fused(): pl.pallas_call(functools.partial(kernel, n_rows, n_cols, depth), out_shap...]
    unnamed x1 -> x0, blocking collectives: 40.6 us -> none
    psum x1 -> x0, blocking collectives: 38.9 us -> none  [local(): lax.psum((jnp.sum(jnp.abs(latest_gate), axis=0), jnp.sum(jnp.abs(latest_u...]
    unnamed x14 -> x0, local copies, waits for them, and re-layouts: 17.2 us -> none
    squeeze x0 -> x2, local copies, waits for them, and re-layouts: none -> 8.76 us  [the longest x1 6.48 us: fused(): ready[1]]
    reduce_sum x1 -> x0, other arithmetic: 8.17 us -> none  [local(): jnp.sum(jnp.abs(latest_up), axis=0)]
    convert_element_type x3 -> x1, other arithmetic: 3.92 us -> 0.59 us  [fused(): served.reshape(-1).astype(jnp.bfloat16)]
  transfers between devices with their start and end apart: 2 -> 0, of which waited for: 2 -> 0; matrix products, arithmetic and copies ran while one was open for 1% -> 0% of each run, Pallas kernels for 0% -> 0%
where the time goes in v1:
time: 190 us; the launch traced here: 189 us
  Pallas kernels  178 us (94%)
  local copies, waits for them, and re-layouts  9.96 us (5%)
    pallas_call x1, Pallas kernels, fused(): pl.pallas_call(functools.partial(kernel, n_rows, n_cols, depth), out_shap...  178 us
    squeeze x1, local copies, waits for them, and re-layouts, fused(): ready[1]  6.48 us

profile of v1, /device:TPU:0, one launch (start us, length us, event | category | flops | bytes accessed | tf_op | source)
XLA Modules:
  0.0 189.5 jit_solution(6829038327604568545)
XLA Ops:
  0.6 0.7 add.3
  1.3 0.1 pad_maximum_fusion
  1.4 0.6 broadcast_in_dim.2.norm_ref
  2.0 177.5 %fused.1 = (bf16[2,2048,2048]{2,1,0:T(8,128)(2,1)S(1)}, f32[2,1,2048]{2,1,0:T(1,128)S(1)}, f32[16,128]{1,0:T(8,128)S(1)}, f32[2,256,2048]{2,1,0:T(8,128)S(1)}) custom-call(f32[256,2048]{1,0:T(8,128)} %w_g.1, f32[256,2048]{1,0:T(8,128)} %f_g.1, f32[256,2048]{1,0:T(8,128)} %s_g.1, f32[256,2048]{1,0:T(8,128)} %w_u.1, f32[256,2048]{1,0:T(8,128)} %f_u.1, ...), custom_call_target="tpu_custom_call" | custom-call | tf_op jit(solution)/shard_map/fused/pallas_call | solution.py:285
  179.5 6.5 %slice_bitcast_fusion = (bf16[2048,2048]{1,0:T(8,128)(2,1)}, bf16[2048,2048]{1,0:T(8,128)(2,1)}) fusion(bf16[2,2048,2048]{2,1,0:T(8,128)(2,1)S(1)} %get-tuple-element.11), kind=kLoop, calls=%fused_computation | loop fusion | bytes 33554432 | tf_op jit(solution)/shard_map/squeeze | solution.py:313
  186.0 0.6 convert_bitcast_fusion
  186.6 0.6 fusion
  187.2 2.3 %slice_bitcast_fusion.2 = (f32[256,2048]{1,0:T(8,128)}, f32[256,2048]{1,0:T(8,128)}) fusion(f32[2,256,2048]{2,1,0:T(8,128)S(1)} %get-tuple-element.14), kind=kLoop, calls=%fused_computation.2 | loop fusion | bytes 8388608 | tf_op jit(solution)/shard_map/squeeze | solution.py:314

commit v2 on v1

--- a/solution.py
+++ b/solution.py
@@ -13,8 +13,8 @@
 decay_rate = 0.1
 tiny_value = 1e-08
 
-PARTS = 4
-SLAB = 32
+PARTS = 8
+SLAB = 64
 
 
 def stepped(w, first, second):
@@ -23,9 +23,10 @@
 
 def kernel(
     n_rows, n_cols, depth,
-    w_g, f_g, s_g, w_u, f_u, s_u, norm_ref,
+    w_g, f_g, s_g, w_u, f_u, s_u, norm_a, norm_b,
     ready, column, served, latest,
-    held, sums, norms, in_sem, sum_send, sum_recv, norm_send, norm_recv, send_sem, recv_sem,
+    held, sums, norms, in_sem, sum_send, sum_recv, norm_send, norm_recv, group_send, group_recv,
+    send_sem, recv_sem,
 ):
     row, col = lax.axis_index("rows"), lax.axis_index("cols")
     z, y = row // 2, lax.rem(row, 2)
@@ -36,7 +37,6 @@
     far_in_z, far_out_z = 2 - half, 3 - half * 3
     share, width = latest.shape[1], latest.shape[2] // PARTS
     pieces = 2 * PARTS
-    devices = n_rows * n_cols
     me = row * n_cols + col
     sources = ((w_g, f_g, s_g), (w_u, f_u, s_u))
 
@@ -60,18 +60,31 @@
 
     barrier = pltpu.get_barrier_semaphore()
 
-    def greet(i, carry):
-        other = lax.rem(me + i, devices)
-        pl.semaphore_signal(
-            barrier, inc=1, device_id=(other // n_cols, lax.rem(other, n_cols)), device_id_type=MESH
-        )
-        return carry
-
-    lax.fori_loop(1, devices, greet, 0)
-
-    lane = lax.broadcasted_iota(jnp.int32, norm_ref.shape, 1)
-    low, high = lax.rem(me, 2) * 64, lax.rem(me, 2) * 64 + 64
-    norms[me] = jnp.where((lane >= low) & (lane < high), norm_ref[...], 0.0)
+    def loop(lo, hi, f):
+        def body(i, carry):
+            f(i)
+            return carry
+
+        lax.fori_loop(lo, hi, body, 0)
+
+    def row_peer(i):
+        return lax.rem(row + i, n_rows)
+
+    def col_peer(i):
+        return lax.rem(col + i, n_cols)
+
+    for i in range(1, n_rows):
+        pl.semaphore_signal(barrier, inc=1, device_id=(row_peer(i), col), device_id_type=MESH)
+    for i in range(1, n_cols):
+        pl.semaphore_signal(barrier, inc=1, device_id=(row, col_peer(i)), device_id_type=MESH)
+
+    lanes = norm_a.shape[1]
+    norms[row, col] = jnp.zeros((1, 2 * lanes), jnp.float32)
+    for side in range(2):
+
+        @pl.when(lax.rem(me, 2) == side)
+        def _():
+            norms[row, col, :, side * lanes : (side + 1) * lanes] = norm_a[...] + norm_b[...]
 
     def adam(k):
         for c in load(k):
@@ -147,7 +160,7 @@
         def _():
             block(row, k, 2, 0, far_near).start()
 
-    LAG = 2
+    LAG = 4
     for k in range(pieces + LAG + 2):
         if k < pieces:
             if k + 2 < pieces:
@@ -155,7 +168,7 @@
                     c.start()
             adam(k)
         if k == 1:
-            pl.semaphore_wait(barrier, devices - 1)
+            pl.semaphore_wait(barrier, n_rows + n_cols - 2)
         if 1 <= k <= pieces:
             for i in range(1, n_rows):
                 sum_copy(k - 1, i).start()
@@ -164,30 +177,28 @@
         if 0 <= k - 2 - LAG:
             send_own(k - 2 - LAG)
 
-    def norm_copy(i):
-        other = lax.rem(me + i, devices)
-        return pltpu.make_async_remote_copy(
-            src_ref=norms.at[me], dst_ref=norms.at[me],
-            send_sem=norm_send.at[other], recv_sem=norm_recv.at[me],
-            device_id=(other // n_cols, lax.rem(other, n_cols)), device_id_type=MESH,
-        )
-
-    def norm_arrival(i):
-        other = lax.rem(me + i, devices)
-        return pltpu.make_async_remote_copy(
-            src_ref=norms.at[other], dst_ref=norms.at[other],
-            send_sem=norm_send.at[other], recv_sem=norm_recv.at[other],
-            device_id=(other // n_cols, lax.rem(other, n_cols)), device_id_type=MESH,
-        )
-
-    def loop(lo, hi, f):
-        def body(i, carry):
-            f(i)
-            return carry
-
-        lax.fori_loop(lo, hi, body, 0)
-
-    loop(1, devices, lambda i: norm_copy(i).start())
+    def norm_copy(i, mine):
+        at = col if mine else col_peer(i)
+        return pltpu.make_async_remote_copy(
+            src_ref=norms.at[row, at], dst_ref=norms.at[row, at],
+            send_sem=norm_send.at[i], recv_sem=norm_recv.at[at],
+            device_id=(row, col_peer(i)), device_id_type=MESH,
+        )
+
+    def group_copy(i, mine):
+        at = row if mine else row_peer(i)
+        return pltpu.make_async_remote_copy(
+            src_ref=norms.at[at], dst_ref=norms.at[at],
+            send_sem=group_send.at[i], recv_sem=group_recv.at[at],
+            device_id=(row_peer(i), col), device_id_type=MESH,
+        )
+
+    for i in range(1, n_cols):
+        norm_copy(i, True).start()
+    for i in range(1, n_cols):
+        norm_copy(i, False).wait_recv()
+    for i in range(1, n_rows):
+        group_copy(i, True).start()
 
     @pl.when(is_outer)
     def _():
@@ -268,50 +279,93 @@
 
     for k in range(pieces):
         loop(1, n_rows, lambda i: sum_copy(k, i).wait_send())
-    loop(1, devices, lambda i: (norm_copy(i).wait_send(), norm_arrival(i).wait_recv()))
-    for i in range(devices // 2):
-        served[pl.ds(i, 1), :] = norms[2 * i][0:1] + norms[2 * i + 1][0:1]
+    for i in range(1, n_cols):
+        norm_copy(i, True).wait_send()
+    for i in range(1, n_rows):
+        group_copy(i, True).wait_send()
+        group_copy(i, False).wait_recv()
+    pairs = n_cols // 2
+    for i in range(n_rows * pairs):
+        r, c = i // pairs, 2 * (i % pairs)
+        served[pl.ds(i, 1), :] = norms[r, c] + norms[r, c + 1]
+
+
+def finish(ready, column, served, latest, *rest):
+    outs, narrow, sem = rest[:7], rest[7], rest[8]
+    narrow[...] = served[...].astype(jnp.bfloat16)
+    copies = []
+    cuts = 4
+    rows = ready.shape[1] // cuts
+    for w in range(2):
+        for i in range(cuts):
+            at = pl.ds(i * rows, rows)
+            copies.append((ready.at[w, at], outs[w].at[at]))
+        copies.append((latest.at[w], outs[5 + w]))
+        copies.append((column.at[w], outs[2 + w]))
+    copies.append((narrow, outs[4]))
+    started = [pltpu.make_async_copy(a, b, sem.at[i]) for i, (a, b) in enumerate(copies)]
+    for c in started:
+        c.start()
+    for c in started:
+        c.wait()
 
 
 def fused(n_rows, n_cols, w_gate, first_gate, second_gate, w_up, first_up, second_up, norm_train, norm_step):
     share, width = w_gate.shape
     depth = share * n_rows
     pieces = 2 * PARTS
-    devices = n_rows * n_cols
-    norm = norm_train + norm_step
-    norm = jnp.broadcast_to(jnp.concatenate([norm, norm])[None, :], (8, 128))
+    lines = n_rows * n_cols // 2
+    lanes = norm_train.shape[0]
     vmem = pl.BlockSpec(memory_space=pltpu.VMEM)
+    hbm = pl.BlockSpec(memory_space=pltpu.HBM)
     dma = pltpu.SemaphoreType.DMA
-    ready, column, served, latest = pl.pallas_call(
+    found = pl.pallas_call(
         functools.partial(kernel, n_rows, n_cols, depth),
         out_shape=[
             pltpu.VMEM((2, depth, width), jnp.bfloat16),
             pltpu.VMEM((2, 1, width), jnp.float32),
-            pltpu.VMEM((devices // 2, 128), jnp.float32),
+            pltpu.VMEM((lines, 2 * lanes), jnp.float32),
             pltpu.VMEM((2, share, width), jnp.float32),
         ],
-        in_specs=[pl.BlockSpec(memory_space=pltpu.HBM)] * 6 + [vmem],
+        in_specs=[hbm] * 6 + [vmem] * 2,
         out_specs=[vmem] * 4,
         scratch_shapes=[
             pltpu.VMEM((3, 2, share, width), jnp.float32),
             pltpu.VMEM((pieces, n_rows, 1, width // PARTS), jnp.float32),
-            pltpu.VMEM((devices, 8, 128), jnp.float32),
+            pltpu.VMEM((n_rows, n_cols, 1, 2 * lanes), jnp.float32),
             dma((3, pieces)),
             dma((pieces, n_rows)),
             dma((pieces, n_rows)),
-            dma((devices,)),
-            dma((devices,)),
+            dma((n_cols,)),
+            dma((n_cols,)),
+            dma((n_rows,)),
+            dma((n_rows,)),
             dma((3, 4, pieces)),
             dma((n_rows, pieces)),
         ],
         compiler_params=pltpu.CompilerParams(
-            collective_id=0, has_side_effects=True, vmem_limit_bytes=40 * 2**20
+            collective_id=0, has_side_effects=True, vmem_limit_bytes=36 * 2**20
         ),
         name="fused",
-    )(w_gate, first_gate, second_gate, w_up, first_up, second_up, norm)
+    )(
+        w_gate, first_gate, second_gate, w_up, first_up, second_up,
+        norm_train.reshape(1, -1), norm_step.reshape(1, -1),
+    )
+    ready_gate, ready_up, column_gate, column_up, served, latest_gate, latest_up = pl.pallas_call(
+        finish,
+        out_shape=[jax.ShapeDtypeStruct((depth, width), jnp.bfloat16)] * 2
+        + [jax.ShapeDtypeStruct((1, width), jnp.float32)] * 2
+        + [jax.ShapeDtypeStruct((lines, 2 * lanes), jnp.bfloat16)]
+        + [jax.ShapeDtypeStruct((share, width), jnp.float32)] * 2,
+        in_specs=[vmem] * 4,
+        out_specs=[hbm] * 7,
+        scratch_shapes=[pltpu.VMEM((lines, 2 * lanes), jnp.bfloat16), dma((13,))],
+        compiler_params=pltpu.CompilerParams(vmem_limit_bytes=2**20),
+        name="finish",
+    )(*found)
     return (
-        ready[0], ready[1], column[0, 0], column[1, 0],
-        served.reshape(-1).astype(jnp.bfloat16), latest[0], latest[1],
+        ready_gate, ready_up, column_gate.reshape(-1), column_up.reshape(-1), served.reshape(-1),
+        latest_gate, latest_up,
     )
 
 

time: 190 us -> 185 us (0.974)
  local copies, waits for them, and re-layouts: 9.96 us -> 0 us
  Pallas kernels: 178 us -> 184 us
    squeeze x2 -> x0, local copies, waits for them, and re-layouts: 8.76 us -> none  [the longest x1 6.48 us: fused(): ready[1]]
    pallas_call x0 -> x1, Pallas kernels: none -> 7.24 us  [fused(): pl.pallas_call(finish, out_shape=[jax.ShapeDtypeStruct((depth, width), jn...]
where the time goes in v2:
time: 185 us
  Pallas kernels  184 us (99%)
    pallas_call x1, Pallas kernels, fused(): pl.pallas_call(functools.partial(kernel, n_rows, n_cols, depth), out_shap...  177 us
    pallas_call x1, Pallas kernels, fused(): pl.pallas_call(finish, out_shape=[jax.ShapeDtypeStruct((depth, width), jn...  7.24 us

profile of v2, /device:TPU:0, one launch (start us, length us, event | category | flops | bytes accessed | tf_op | source)
XLA Modules:
  0.0 185.0 jit_solution(7527705856010529758)
XLA Ops:
  0.6 177.1 %fused.1 = (bf16[2,2048,2048]{2,1,0:T(8,128)(2,1)S(1)}, f32[2,1,2048]{2,1,0:T(1,128)S(1)}, f32[16,128]{1,0:T(8,128)S(1)}, f32[2,256,2048]{2,1,0:T(8,128)S(1)}) custom-call(f32[256,2048]{1,0:T(8,128)} %w_g.1, f32[256,2048]{1,0:T(8,128)} %f_g.1, f32[256,2048]{1,0:T(8,128)} %s_g.1, f32[256,2048]{1,0:T(8,128)} %w_u.1, f32[256,2048]{1,0:T(8,128)} %f_u.1, ...), custom_call_target="tpu_custom_call" | custom-call | tf_op jit(solution)/shard_map/fused/pallas_call | solution.py:322
  177.7 7.2 %finish.1 = (bf16[2048,2048]{1,0:T(8,128)(2,1)}, bf16[2048,2048]{1,0:T(8,128)(2,1)}, f32[1,2048]{1,0:T(1,128)}, f32[1,2048]{1,0:T(1,128)}, bf16[16,128]{1,0:T(8,...) custom-call(bf16[2,2048,2048]{2,1,0:T(8,128)(2,1)S(1)} %get-tuple-element.18.ready, ...), custom_call_target="tpu_custom_call" | custom-call | tf_op jit(solution)/shard_map/finish/pallas_call | solution.py:354

commit v3 on v2

--- a/solution.py
+++ b/solution.py
@@ -14,6 +14,7 @@
 tiny_value = 1e-08
 
 PARTS = 8
+LATE = 2
 SLAB = 64
 
 
@@ -24,7 +25,7 @@
 def kernel(
     n_rows, n_cols, depth,
     w_g, f_g, s_g, w_u, f_u, s_u, norm_a, norm_b,
-    ready, column, served, latest,
+    ready, column, served, latest, late,
     held, sums, norms, in_sem, sum_send, sum_recv, norm_send, norm_recv, group_send, group_recv,
     send_sem, recv_sem,
 ):
@@ -161,7 +162,7 @@
             block(row, k, 2, 0, far_near).start()
 
     LAG = 4
-    for k in range(pieces + LAG + 2):
+    for k in range(pieces + LAG + 1):
         if k < pieces:
             if k + 2 < pieces:
                 for c in load(k + 2):
@@ -169,13 +170,13 @@
             adam(k)
         if k == 1:
             pl.semaphore_wait(barrier, n_rows + n_cols - 2)
+        if 0 <= k - 1 - LAG:
+            scale(k - 1 - LAG)
         if 1 <= k <= pieces:
             for i in range(1, n_rows):
                 sum_copy(k - 1, i).start()
-        if LAG <= k - 1 < pieces + LAG:
-            scale(k - 1 - LAG)
-        if 0 <= k - 2 - LAG:
-            send_own(k - 2 - LAG)
+        if 0 <= k - 1 - LAG:
+            send_own(k - 1 - LAG)
 
     def norm_copy(i, mine):
         at = col if mine else col_peer(i)
@@ -200,6 +201,10 @@
     for i in range(1, n_rows):
         group_copy(i, True).start()
 
+    def keep(source):
+        at = pl.ds(pl.multiple_of(source * share, share), share)
+        late[...] = ready[1, at, (PARTS - LATE) * width : PARTS * width]
+
     @pl.when(is_outer)
     def _():
         def one(k):
@@ -222,15 +227,24 @@
 
         def three(k):
             arrived(far_away, k)
-            block(far_away, k, 0, 3, across).start()
+
+            @pl.when(k < pieces - LATE)
+            def _():
+                block(far_away, k, 0, 3, across).start()
 
         loop(0, pieces, three)
+        keep(far_away)
 
         def rest(k):
-            arrived(near_across, k)
             arrived(far_near_across, k)
-            arrived(far_away_across, k)
-            for slot in (0, 2, 3):
+
+            @pl.when(k < pieces - LATE)
+            def _():
+                arrived(near_across, k)
+                arrived(far_away_across, k)
+                block(row, k, 0, 3, across).wait_send()
+
+            for slot in (0, 2):
                 block(row, k, 0, slot, across).wait_send()
             for slot in (0, 1):
                 block(row, k, 1, slot, near).wait_send()
@@ -259,7 +273,8 @@
             block(far_away, k, 0, 1, across).start()
 
         loop(0, pieces, two)
-        loop(PARTS, pieces, lambda k: block(across, k, 1, 3, away).start())
+        loop(PARTS, pieces - LATE, lambda k: block(across, k, 1, 3, away).start())
+        keep(across)
 
         def rest(k):
             arrived(away_across, k)
@@ -271,7 +286,7 @@
                 block(row, k, 1, slot, away).wait_send()
                 block(row, k, 2, slot, far_near).wait_send()
 
-            @pl.when(k >= PARTS)
+            @pl.when((k >= PARTS) & (k < pieces - LATE))
             def _():
                 block(row, k, 1, 3, away).wait_send()
 
@@ -310,6 +325,25 @@
         c.wait()
 
 
+def place(from_z, from_y, old, new, sem):
+    row = lax.axis_index("rows")
+    z, y = row // 2, lax.rem(row, 2)
+    half = z // 2
+    share, width = from_z.shape
+
+    @pl.when(lax.rem(z + half, 2) == 0)
+    def _():
+        copies = []
+        for i, (ref, at_z) in enumerate(((from_z, 1 + half), (from_y, 3 - half * 3))):
+            start = pl.multiple_of((at_z * 2 + 1 - y) * share, share)
+            to = new.at[pl.ds(start, share), pl.ds(new.shape[1] - width, width)]
+            copies.append(pltpu.make_async_copy(ref, to, sem.at[i]))
+        for c in copies:
+            c.start()
+        for c in copies:
+            c.wait()
+
+
 def fused(n_rows, n_cols, w_gate, first_gate, second_gate, w_up, first_up, second_up, norm_train, norm_step):
     share, width = w_gate.shape
     depth = share * n_rows
@@ -319,16 +353,17 @@
     vmem = pl.BlockSpec(memory_space=pltpu.VMEM)
     hbm = pl.BlockSpec(memory_space=pltpu.HBM)
     dma = pltpu.SemaphoreType.DMA
-    found = pl.pallas_call(
+    *found, late = pl.pallas_call(
         functools.partial(kernel, n_rows, n_cols, depth),
         out_shape=[
             pltpu.VMEM((2, depth, width), jnp.bfloat16),
             pltpu.VMEM((2, 1, width), jnp.float32),
             pltpu.VMEM((lines, 2 * lanes), jnp.float32),
             pltpu.VMEM((2, share, width), jnp.float32),
+            pltpu.VMEM((share, LATE * (width // PARTS)), jnp.bfloat16),
         ],
         in_specs=[hbm] * 6 + [vmem] * 2,
-        out_specs=[vmem] * 4,
+        out_specs=[vmem] * 5,
         scratch_shapes=[
             pltpu.VMEM((3, 2, share, width), jnp.float32),
             pltpu.VMEM((pieces, n_rows, 1, width // PARTS), jnp.float32),
@@ -351,6 +386,9 @@
         w_gate, first_gate, second_gate, w_up, first_up, second_up,
         norm_train.reshape(1, -1), norm_step.reshape(1, -1),
     )
+    last = n_rows - 1
+    from_z = lax.ppermute(late, "rows", [(2, 0), (3, 1), (last - 3, last - 1), (last - 2, last)])
+    from_y = lax.ppermute(late, "rows", [(0, 1), (1, 0), (last - 1, last), (last, last - 1)])
     ready_gate, ready_up, column_gate, column_up, served, latest_gate, latest_up = pl.pallas_call(
         finish,
         out_shape=[jax.ShapeDtypeStruct((depth, width), jnp.bfloat16)] * 2
@@ -361,8 +399,19 @@
         out_specs=[hbm] * 7,
         scratch_shapes=[pltpu.VMEM((lines, 2 * lanes), jnp.bfloat16), dma((13,))],
         compiler_params=pltpu.CompilerParams(vmem_limit_bytes=2**20),
+        cost_estimate=pl.CostEstimate(flops=0, bytes_accessed=40 * 2**20, transcendentals=0),
         name="finish",
     )(*found)
+    ready_up = pl.pallas_call(
+        place,
+        out_shape=jax.ShapeDtypeStruct((depth, width), jnp.bfloat16),
+        in_specs=[vmem] * 2 + [hbm],
+        out_specs=hbm,
+        input_output_aliases={2: 0},
+        scratch_shapes=[dma((2,))],
+        compiler_params=pltpu.CompilerParams(vmem_limit_bytes=2**20),
+        name="place",
+    )(from_z, from_y, ready_up)
     return (
         ready_gate, ready_up, column_gate.reshape(-1), column_up.reshape(-1), served.reshape(-1),
         latest_gate, latest_up,

time: 185 us -> 185 us (level)
  Pallas kernels: 184 us -> 179 us
  starting transfers between devices: 0 us -> 4.37 us
    pallas_call x1, Pallas kernels: 177 us -> 171 us  [fused(): pl.pallas_call(functools.partial(kernel, n_rows, n_cols, depth), out_shap...]
    ppermute x0 -> x2, starting transfers between devices: none -> 4.37 us  [the longest x1 3.08 us: fused(): lax.ppermute(late, 'rows', [(0, 1), (1, 0), (last - 1, last), (last, last...]
  transfers between devices with their start and end apart: 0 -> 2, of which waited for: 0 -> 0; matrix products, arithmetic and copies ran while one was open for 0% -> 0% of each run, Pallas kernels for 0% -> 4%
where the time goes in v3:
time: 185 us
  Pallas kernels  179 us (97%)
  starting transfers between devices  4.37 us (2%)
    pallas_call x1, Pallas kernels, fused(): pl.pallas_call(functools.partial(kernel, n_rows, n_cols, depth), out_shap...  171 us
    pallas_call x1, Pallas kernels, fused(): pl.pallas_call(finish, out_shape=[jax.ShapeDtypeStruct((depth, width), jn...  7.24 us
  transfers between devices with their start and end apart: 2, of which 0 were waited for; matrix products, arithmetic and copies ran while one was open for 0% of the time, Pallas kernels for 4%

profile of v3, /device:TPU:0, one launch (start us, length us, event | category | flops | bytes accessed | tf_op | source)
XLA Modules:
  0.0 184.5 jit_solution(6232440824109141406)
XLA Ops:
  0.6 171.4 %fused.1 = (bf16[2,2048,2048]{2,1,0:T(8,128)(2,1)S(1)}, f32[2,1,2048]{2,1,0:T(1,128)S(1)}, f32[16,128]{1,0:T(8,128)S(1)}, f32[2,256,2048]{2,1,0:T(8,128)S(1)}, bf16[256,512]{1,0:T(8,128)(2,1)S(1)}) custom-call(f32[256,2048]{1,0:T(8,128)} %w_g.1, f32[256,2048]{1,0:T(8,128)} %f_g.1, f32[256,2048]{1,0:T(8,128)} %s_g.1, f32[256,2048]{1,0:T(8,128)} %w_u.1, ...), custom_call_target="tpu_custom_call" | custom-call | tf_op jit(solution)/shard_map/fused/pallas_call | solution.py:356
  172.0 3.1 %collective-permute-start.1 = (bf16[256,512]{1,0:T(8,128)(2,1)S(1)}, bf16[256,512]{1,0:T(8,128)(2,1)S(1)}, u32[]{:S(2)}, u32[]{:S(2)}) collective-permute-start(bf16[256,512]{1,0:T(8,128)(2,1)S(1)} %get-tuple-element.24), channel_id=1, source_target_pairs={{0,4},{4,0},{24,28},{28,24},{1,5},{5,1},{25,29},{29,25},{2,6},{6,2... | collective-permute-start | bytes 786440 | tf_op jit(solution)/shard_map/ppermute | solution.py:391
  175.1 1.3 collective-permute-start
  176.4 7.2 %finish.1 = (bf16[2048,2048]{1,0:T(8,128)(2,1)}, bf16[2048,2048]{1,0:T(8,128)(2,1)}, f32[1,2048]{1,0:T(1,128)}, f32[1,2048]{1,0:T(1,128)}, bf16[16,128]{1,0:T(8,...) custom-call(bf16[2,2048,2048]{2,1,0:T(8,128)(2,1)S(1)} %get-tuple-element.19.ready, ...), custom_call_target="tpu_custom_call" | custom-call | bytes 41943040 | tf_op jit(solution)/shard_map/finish/pallas_call | solution.py:392
  183.7 0.0 collective-permute-done.1.from_y
  183.7 0.0 collective-permute-done.from_z
  183.7 0.8 place.1
Async XLA Ops:
  172.0 11.6 %collective-permute-start.1 = (bf16[256,512]{1,0:T(8,128)(2,1)S(1)}, bf16[256,512]{1,0:T(8,128)(2,1)S(1)}, u32[]{:S(2)}, u32[]{:S(2)}) collective-permute-start(bf16[256,512]{1,0:T(8,128)(2,1)S(1)} %get-tuple-element.24), channel_id=1, source_target_pairs={{0,4},{4,0},{24,28},{28,24},{1,5},{5,1},{25,29},{29,25},{2,6},{6,2... | collective-permute-start | bytes 786440 | tf_op jit(solution)/shard_map/ppermute | solution.py:391
  175.1 8.6 %collective-permute-start = (bf16[256,512]{1,0:T(8,128)(2,1)S(1)}, bf16[256,512]{1,0:T(8,128)(2,1)S(1)}, u32[]{:S(2)}, u32[]{:S(2)}) collective-permute-start(bf16[256,512]{1,0:T(8,128)(2,1)S(1)} %get-tuple-element.24), channel_id=1, source_target_pairs={{8,0},{12,4},{16,24},{20,28},{9,1},{13,5},{17,25},{21,29},{10,2},{... | collective-permute-start | bytes 786440 | tf_op jit(solution)/shard_map/ppermute | solution.py:390

commit v4 on v3

--- a/solution.py
+++ b/solution.py
@@ -14,7 +14,7 @@
 tiny_value = 1e-08
 
 PARTS = 8
-LATE = 2
+LATE = 3
 SLAB = 64
 
 

time: 185 us -> 185 us (level)
  waiting for transfers between devices: 0.01 us -> 2.55 us
  Pallas kernels: 179 us -> 177 us
    pallas_call x1, Pallas kernels: 171 us -> 169 us  [fused(): pl.pallas_call(functools.partial(kernel, n_rows, n_cols, depth), out_shap...]
    ppermute x1, waiting for transfers between devices: 0.01 us -> 2.54 us  [fused(): lax.ppermute(late, 'rows', [(2, 0), (3, 1), (last - 3, last - 1), (last -...]
  transfers between devices with their start and end apart: 2 -> 2, of which waited for: 0 -> 1; matrix products, arithmetic and copies ran while one was open for 0% -> 0% of each run, Pallas kernels for 4% -> 4%
where the time goes in v4:
time: 185 us; the launch traced here: 184 us
  Pallas kernels  177 us (96%)
  starting transfers between devices  4.37 us (2%)
  waiting for transfers between devices  2.55 us (1%)
    pallas_call x1, Pallas kernels, fused(): pl.pallas_call(functools.partial(kernel, n_rows, n_cols, depth), out_shap...  169 us
    pallas_call x1, Pallas kernels, fused(): pl.pallas_call(finish, out_shape=[jax.ShapeDtypeStruct((depth, width), jn...  7.24 us
  transfers between devices with their start and end apart: 2, of which 1 were waited for; matrix products, arithmetic and copies ran while one was open for 0% of the time, Pallas kernels for 4%

profile of v4, /device:TPU:0, one launch (start us, length us, event | category | flops | bytes accessed | tf_op | source)
XLA Modules:
  0.0 184.4 jit_solution(14146728334092207228)
XLA Ops:
  0.6 168.6 %fused.1 = (bf16[2,2048,2048]{2,1,0:T(8,128)(2,1)S(1)}, f32[2,1,2048]{2,1,0:T(1,128)S(1)}, f32[16,128]{1,0:T(8,128)S(1)}, f32[2,256,2048]{2,1,0:T(8,128)S(1)}, bf16[256,768]{1,0:T(8,128)(2,1)S(1)}) custom-call(f32[256,2048]{1,0:T(8,128)} %w_g.1, f32[256,2048]{1,0:T(8,128)} %f_g.1, f32[256,2048]{1,0:T(8,128)} %s_g.1, f32[256,2048]{1,0:T(8,128)} %w_u.1, ...), custom_call_target="tpu_custom_call" | custom-call | tf_op jit(solution)/shard_map/fused/pallas_call | solution.py:356
  169.3 3.1 %collective-permute-start.1 = (bf16[256,768]{1,0:T(8,128)(2,1)S(1)}, bf16[256,768]{1,0:T(8,128)(2,1)S(1)}, u32[]{:S(2)}, u32[]{:S(2)}) collective-permute-start(bf16[256,768]{1,0:T(8,128)(2,1)S(1)} %get-tuple-element.24), channel_id=1, source_target_pairs={{0,4},{4,0},{24,28},{28,24},{1,5},{5,1},{25,29},{29,25},{2,6},{6,2... | collective-permute-start | bytes 1179656 | tf_op jit(solution)/shard_map/ppermute | solution.py:391
  172.4 1.3 collective-permute-start
  173.7 7.2 %finish.1 = (bf16[2048,2048]{1,0:T(8,128)(2,1)}, bf16[2048,2048]{1,0:T(8,128)(2,1)}, f32[1,2048]{1,0:T(1,128)}, f32[1,2048]{1,0:T(1,128)}, bf16[16,128]{1,0:T(8,...) custom-call(bf16[2,2048,2048]{2,1,0:T(8,128)(2,1)S(1)} %get-tuple-element.19.ready, ...), custom_call_target="tpu_custom_call" | custom-call | bytes 41943040 | tf_op jit(solution)/shard_map/finish/pallas_call | solution.py:392
  180.9 0.0 collective-permute-done.1.from_y
  180.9 2.5 %collective-permute-done.from_z = bf16[256,768]{1,0:T(8,128)(2,1)S(1)} collective-permute-done((bf16[256,768]{1,0:T(8,128)(2,1)S(1)}, bf16[256,768]{1,0:T(8,128)(2,1)S(1)}, u32[]{:S(2)}, u32[]{:S(2)}) %collective-permute-start) | collective-permute-done | bytes 393248 | tf_op jit(solution)/shard_map/ppermute | solution.py:390
  183.5 0.9 place.1
Async XLA Ops:
  169.3 11.6 %collective-permute-start.1 = (bf16[256,768]{1,0:T(8,128)(2,1)S(1)}, bf16[256,768]{1,0:T(8,128)(2,1)S(1)}, u32[]{:S(2)}, u32[]{:S(2)}) collective-permute-start(bf16[256,768]{1,0:T(8,128)(2,1)S(1)} %get-tuple-element.24), channel_id=1, source_target_pairs={{0,4},{4,0},{24,28},{28,24},{1,5},{5,1},{25,29},{29,25},{2,6},{6,2... | collective-permute-start | bytes 1179656 | tf_op jit(solution)/shard_map/ppermute | solution.py:391
  172.4 11.1 %collective-permute-start = (bf16[256,768]{1,0:T(8,128)(2,1)S(1)}, bf16[256,768]{1,0:T(8,128)(2,1)S(1)}, u32[]{:S(2)}, u32[]{:S(2)}) collective-permute-start(bf16[256,768]{1,0:T(8,128)(2,1)S(1)} %get-tuple-element.24), channel_id=1, source_target_pairs={{8,0},{12,4},{16,24},{20,28},{9,1},{13,5},{17,25},{21,29},{10,2},{... | collective-permute-start | bytes 1179656 | tf_op jit(solution)/shard_map/ppermute | solution.py:390
